TPU v7x, 256 devices: a 4x2x16 block of a 4x16x16 slice. The times are simulated.
256 devices in a mesh: groups: 2 (over y), ep: 32 (over z, core), sub: 4 (over x).
Axes of the slice: x: 4, y: 2, z: 16, core: 2. Of those that a mesh axis runs over, the one named last changes fastest.
The devices are a block of a 4x16x16 slice.
Arguments:
- tokens: bfloat16 [4096, 7168], P(('groups', 'ep'), 'sub'), parts along dimension 0, may hold values from -6 to 6
- expert_ids: int32 [4096, 8], P(('groups', 'ep')), parts along dimension 0, may hold values from 0 to 31, all different within a row; in each aligned block of 64 rows (0 to 63, 64 to 127, ...) at most 24 rows name the same one
- route_weights: float32 [4096, 8], P(('groups', 'ep')), parts along dimension 0, may hold values from 0.05 to 0.6
- gate_weight: bfloat16 [32, 7168, 1024], P('ep', 'sub'), may hold values from -0.0625 to 0.0625
- up_weight: bfloat16 [32, 7168, 1024], P('ep', 'sub'), may hold values from -0.0625 to 0.0625
- down_weight: bfloat16 [32, 1024, 7168], P('ep', None, 'sub'), may hold values from -0.1875 to 0.1875
- shared_gate: bfloat16 [1024, 7168], P('ep', 'sub'), may hold values from -0.0625 to 0.0625
- shared_up: bfloat16 [1024, 7168], P('ep', 'sub'), may hold values from -0.0625 to 0.0625
- shared_down: bfloat16 [1024, 7168], P('ep', 'sub'), may hold values from -0.1875 to 0.1875
Outputs:
- layer_out: bfloat16 [4096, 7168], P(('groups', 'ep'), 'sub'), parts along dimension 0
There are 2 independent parts, one for each index of `groups`. A program takes and returns all parts, laid end to end along the dimension named above; an argument that names none is the same for every part. Nothing has to cross between parts.
Inputs may be any that keep to these rules, and one draw needn't show every extreme that they name: `expert_ids`: each row names 8 different experts. Among the 64 rows of one ep index no expert is named more than 24 times, and in some of these aligned blocks an expert is named exactly 24 times.
All inputs are finite; a program needn't handle non-finite values.
Results may differ from a plain program's by a relative error of at most 0.0054.
Values may be sent and summed in bfloat16 or wider, within the bound.
A program may use at most 128 MiB of HBM per device.

v0:
```python
import jax
import jax.numpy as jnp
from jax import lax
from jax.sharding import PartitionSpec as P


def from_everyone(value, axis):
    copies = jnp.broadcast_to(value, (lax.axis_size(axis), *value.shape))
    return lax.all_to_all(copies, axis, split_axis=0, concat_axis=0, tiled=True)


def joined_along(pieces, dim):
    pieces = jnp.moveaxis(pieces, 0, dim)
    lengths = pieces.shape
    return pieces.reshape(*lengths[:dim], lengths[dim] * lengths[dim + 1], *lengths[dim + 2 :])


def gathered_copies(value, axis, dim):
    pieces = from_everyone(value, axis)
    return joined_along(pieces, dim)


def of_everyone(value, axis):
    return from_everyone(value, axis).sum(axis=0)


def together(arrays, axis):
    ends = [0]
    for a in arrays:
        ends.append(ends[-1] + a.size)
    running = of_everyone(jnp.concatenate([a.ravel() for a in arrays]), axis)
    return tuple((running[b:e].reshape(a.shape) for a, b, e in zip(arrays, ends, ends[1:])))


def per_device(
    tokens,
    expert_ids,
    route_weights,
    gate_weight,
    up_weight,
    down_weight,
    shared_gate,
    shared_up,
    shared_down,
):
    contract = (((1,), (1,)), ((), ()))
    experts_all = lax.axis_size("ep")
    token_count = tokens.shape[0]
    quarter = tokens.shape[1]
    top_count = expert_ids.shape[1]
    capacity = token_count * top_count * 3 // (2 * experts_all)
    choices_flat = expert_ids.reshape(-1)
    one_hot = (choices_flat[:, None] == jnp.arange(experts_all, dtype=jnp.int32)[None, :]).astype(
        jnp.int32
    )
    earlier = jnp.cumsum(one_hot, axis=0) - one_hot
    slot_index = jnp.sum(earlier * one_hot, axis=1)
    target = choices_flat * capacity + slot_index
    target_grid = target.reshape(token_count, top_count)
    slot_ids = jnp.arange(experts_all * capacity, dtype=jnp.int32)
    placing = jnp.any(target_grid[None, :, :] == slot_ids[:, None, None], axis=2).astype(
        jnp.bfloat16
    )
    outgoing = jnp.dot(placing, tokens, preferred_element_type=jnp.float32).astype(jnp.bfloat16)
    outgoing = outgoing.reshape(experts_all, capacity, quarter)
    arrived = lax.all_to_all(outgoing, "ep", split_axis=0, concat_axis=0, tiled=True)
    expert_rows = arrived.reshape(-1, quarter)
    gate_part = jnp.dot(expert_rows, gate_weight[0], preferred_element_type=jnp.float32)
    up_part = jnp.dot(expert_rows, up_weight[0], preferred_element_type=jnp.float32)
    summed = lax.psum_scatter(
        jnp.concatenate([gate_part, up_part], axis=1), "sub", scatter_dimension=0, tiled=True
    )
    hidden_width = summed.shape[1] // 2
    part_hidden = (jax.nn.silu(summed[:, :hidden_width]) * summed[:, hidden_width:]).astype(
        jnp.bfloat16
    )
    expert_hidden = gathered_copies(part_hidden, "sub", 0)
    expert_out = jnp.dot(expert_hidden, down_weight[0], preferred_element_type=jnp.float32).astype(
        jnp.bfloat16
    )
    expert_out = expert_out.reshape(experts_all, capacity, quarter)
    returned = lax.all_to_all(expert_out, "ep", split_axis=0, concat_axis=0, tiled=True)
    gathered = returned.reshape(-1, quarter)[target].reshape(token_count, top_count, quarter)
    routed = jnp.sum(gathered.astype(jnp.float32) * route_weights[:, :, None], axis=1)
    gate_cols = lax.dot_general(
        tokens,
        lax.all_gather(shared_gate, "ep", axis=0, tiled=True),
        contract,
        preferred_element_type=jnp.float32,
    )
    up_cols = lax.dot_general(
        tokens,
        lax.all_gather(shared_up, "ep", axis=0, tiled=True),
        contract,
        preferred_element_type=jnp.float32,
    )
    shared_pre = gate_cols
    shared_lin = up_cols
    shared_pre, shared_lin = together((shared_pre, shared_lin), "sub")
    shared_hidden = (jax.nn.silu(shared_pre) * shared_lin).astype(jnp.bfloat16)
    shared_out = jnp.dot(
        shared_hidden,
        lax.all_gather(shared_down, "ep", axis=0, tiled=True),
        preferred_element_type=jnp.float32,
    )
    return (shared_out + routed).astype(jnp.bfloat16)


def solution(mesh):
    in_specs = (
        P(("groups", "ep"), "sub"),
        P(("groups", "ep"), None),
        P(("groups", "ep"), None),
        P("ep", "sub", None),
        P("ep", "sub", None),
        P("ep", None, "sub"),
        P("ep", "sub"),
        P("ep", "sub"),
        P("ep", "sub"),
    )
    out_specs = P(("groups", "ep"), "sub")
    return jax.shard_map(
        per_device, mesh=mesh, in_specs=in_specs, out_specs=out_specs, check_vma=False
    )
```

profile of v0, /device:TPU:33, one launch (start us, length us, event | category | flops | bytes accessed | tf_op | source)
XLA Modules:
  0.0 494.1 jit_solution(12589480191774770457)
XLA Ops:
  7.4 0.0 copy-start
  7.4 0.0 all-gather.4.cloned.1.call-start
  7.4 0.7 all-gather.4.cloned.1.call-update
  8.2 0.8 copy.23
  8.9 0.1 eq.42
  9.0 0.1 eq.38
  9.1 1.2 reduce-window.6
  10.3 0.2 slice_reduce_fusion
  10.6 0.1 fusion.16
  10.7 0.1 reduce_sum.33
  10.8 0.5 fusion.11
  11.3 0.0 copy-done
  11.3 2.5 convolution_convert_fusion
  13.8 25.5 %all-to-all-start.1 = ((bf16[32,24,1792]{2,1,0:T(8,128)(2,1)}), bf16[32,24,1792]{2,1,0:T(8,128)(2,1)S(1)}, u32[]{:S(2)}, u32[]{:S(2)}) async-start(bf16[32,24,1792]{2,1,0:T(8,128)(2,1)} %bitcast.1), calls=%async_computation.1 | async-start | bytes 5505024 | tf_op jit(solution)/shard_map/all_to_all | solution.py:66
  39.3 0.1 all-gather.6.cloned.1.call-start
  39.4 0.7 all-gather.6.cloned.1.call-update
  40.1 0.1 reduce-scatter.2.cloned.1.call-start
  40.2 141.1 %all-to-all-done.1 = bf16[32,24,1792]{2,1,0:T(8,128)(2,1)S(1)} async-done(((bf16[32,24,1792]{2,1,0:T(8,128)(2,1)}), bf16[32,24,1792]{2,1,0:T(8,128)(2,1)S(1)}, u32[]{:S(2)}, u32[]{:S(2)}) %all-to-all-start.1) | async-done | bytes 2752544 | tf_op jit(solution)/shard_map/all_to_all | solution.py:66
  181.3 0.0 copy-start.4
  181.3 5.2 %fusion.3 = f32[768,1024]{1,0:T(8,128)S(1)} fusion(bf16[768,1792]{1,0:T(8,128)(2,1)S(1)} %bitcast.58, bf16[1,1792,1024]{2,1,0:T(8,128)(2,1)} %param.13), kind=kOutput, calls=%fused_computation.6 | convolution fusion | flops 2818572288 | bytes 9568256 | tf_op jit(solution)/shard_map/dot_general | solution.py:69
  186.5 0.0 copy-done.4
  186.5 3.0 fusion.5
  189.5 3.1 pad_maximum_fusion
  192.6 0.1 reduce-scatter.2.cloned.1.call-update
  192.7 0.0 all-gather.4.cloned.1.call-done
  192.7 3.2 convolution_bitcast_fusion.1
  195.9 0.1 copy.32
  196.0 45.4 %all-gather.6.cloned.1.call-done = bf16[1024,1792]{1,0:T(8,128)(2,1)} async-done(((bf16[32,1792]{1,0:T(8,128)(2,1)}), bf16[1024,1792]{1,0:T(8,128)(2,1)}) %all-gather.6.cloned.1.call-update) | async-done | bytes 3670032 | tf_op jit(solution)/shard_map/all_gather | solution.py:93
  241.4 3.2 convolution_bitcast_fusion
  244.6 0.1 copy.33
  244.7 15.0 %reduce-scatter.2.cloned.1.call-done = f32[192,2048]{1,0:T(8,128)} async-done(((f32[768,2048]{1,0:T(8,128)}), f32[192,2048]{1,0:T(8,128)}) %reduce-scatter.2.cloned.1.call-update) | async-done | bytes 1572880 | tf_op jit(solution)/shard_map/reduce_scatter | solution.py:70
  259.7 1.6 fusion.12
  261.3 1.4 broadcast_in_dim.5
  262.6 3.7 all-to-all-start.2
  266.3 19.9 %all-to-all-done.2 = bf16[4,192,1024]{2,1,0:T(8,128)(2,1)S(1)} async-done(((bf16[4,192,1024]{2,1,0:T(8,128)(2,1)}), bf16[4,192,1024]{2,1,0:T(8,128)(2,1)S(1)}, u32[]{:S(2)}, u32[]{:S(2)}) %all-to-all-start.2) | async-done | bytes 1572896 | tf_op jit(solution)/shard_map/all_to_all | solution.py:9
  286.2 0.0 copy-start.2
  286.2 2.4 broadcast_in_dim.4
  288.6 0.0 copy-done.2
  288.6 3.9 all-to-all-start
  292.5 7.1 %fusion.7 = bf16[768,1792]{1,0:T(8,128)(2,1)} fusion(bf16[768,1024]{1,0:T(8,128)(2,1)} %bitcast.60, bf16[1,1024,1792]{2,1,0:T(8,128)(2,1)} %param.14), kind=kOutput, calls=%fused_computation.10 | convolution fusion | flops 2819948544 | bytes 7995392 | tf_op jit(solution)/shard_map/dot_general | solution.py:78
  299.6 0.0 copy-start.3
  299.6 17.4 %all-to-all-done = f32[4,1,131072]{2,1,0:T(1,128)S(1)} async-done(((f32[4,1,131072]{2,1,0:T(1,128)}), f32[4,1,131072]{2,1,0:T(1,128)S(1)}, u32[]{:S(2)}, u32[]{:S(2)}) %all-to-all-start) | async-done | bytes 2097184 | tf_op jit(solution)/shard_map/all_to_all | solution.py:9
  317.0 0.0 copy-start.1
  317.0 1.3 copy-done.1
  318.4 14.9 %all-to-all-start.3 = ((bf16[32,24,1792]{2,1,0:T(8,128)(2,1)}), bf16[32,24,1792]{2,1,0:T(8,128)(2,1)S(1)}, u32[]{:S(2)}, u32[]{:S(2)}) async-start(bf16[32,24,1792]{2,1,0:T(8,128)(2,1)} %bitcast.57), calls=%async_computation.4 | async-start | bytes 5505024 | tf_op jit(solution)/shard_map/all_to_all | solution.py:82
  333.3 0.1 all-gather.8.cloned.1.call-start
  333.4 0.7 all-gather.8.cloned.1.call-update
  334.1 0.1 mul.50
  334.2 0.0 copy-done.3
  334.2 0.1 copy.27
  334.3 3.5 reduce_sum.31
  337.9 0.9 fusion.20
  338.7 1.0 slice.39
  339.7 1.0 slice.41
  340.7 136.5 %all-to-all-done.3 = bf16[32,24,1792]{2,1,0:T(8,128)(2,1)S(1)} async-done(((bf16[32,24,1792]{2,1,0:T(8,128)(2,1)}), bf16[32,24,1792]{2,1,0:T(8,128)(2,1)S(1)}, u32[]{:S(2)}, u32[]{:S(2)}) %all-to-all-start.3) | async-done | bytes 2752544 | tf_op jit(solution)/shard_map/all_to_all | solution.py:82
  477.2 3.1 gather_fusion
  480.4 3.1 fusion
  483.5 0.0 all-gather.8.cloned.1.call-done
  483.5 3.5 fusion.10
  (7 shorter events, 0.1 us)
Async XLA Ops:
  7.4 3.9 copy-start
  7.4 185.3 %all-gather.4.cloned.1.call-start = ((), (), s32[]{:S(2)}) async-start(), calls=%async_computation.5 | async-start | bytes 3784704 | tf_op jit(solution)/shard_map/all_gather | solution.py:87
  13.8 167.5 %all-to-all-start.1 = ((bf16[32,24,1792]{2,1,0:T(8,128)(2,1)}), bf16[32,24,1792]{2,1,0:T(8,128)(2,1)S(1)}, u32[]{:S(2)}, u32[]{:S(2)}) async-start(bf16[32,24,1792]{2,1,0:T(8,128)(2,1)} %bitcast.1), calls=%async_computation.1 | async-start | bytes 5505024 | tf_op jit(solution)/shard_map/all_to_all | solution.py:66
  39.3 202.0 %all-gather.6.cloned.1.call-start = ((), (), s32[]{:S(2)}) async-start(), calls=%async_computation.6 | async-start | bytes 3784704 | tf_op jit(solution)/shard_map/all_gather | solution.py:93
  40.1 219.5 %reduce-scatter.2.cloned.1.call-start = ((), (), s32[]{:S(2)}) async-start(), calls=%async_computation.8 | async-start | bytes 7864320 | tf_op jit(solution)/shard_map/reduce_scatter | solution.py:70
  181.3 5.2 %copy-start.4 = (bf16[1,1792,1024]{2,1,0:T(8,128)(2,1)S(1)}, bf16[1,1792,1024]{2,1,0:T(8,128)(2,1)}, u32[]{:S(2)}) copy-start(bf16[1,1792,1024]{2,1,0:T(8,128)(2,1)} %param.12) | copy-start | bytes 11010052
  262.6 23.6 %all-to-all-start.2 = ((bf16[4,192,1024]{2,1,0:T(8,128)(2,1)}), bf16[4,192,1024]{2,1,0:T(8,128)(2,1)S(1)}, u32[]{:S(2)}, u32[]{:S(2)}) async-start(bf16[4,192,1024]{2,1,0:T(8,128)(2,1)} %broadcast_in_dim.5), calls=%async_computation.3 | async-start | bytes 3145728 | tf_op jit(solution)/shard_map/all_to_all | solution.py:9
  286.2 2.4 copy-start.2
  288.6 28.4 %all-to-all-start = ((f32[4,1,131072]{2,1,0:T(1,128)}), f32[4,1,131072]{2,1,0:T(1,128)S(1)}, u32[]{:S(2)}, u32[]{:S(2)}) async-start(f32[4,1,131072]{2,1,0:T(1,128)} %broadcast_in_dim.4), calls=%async_computation | async-start | bytes 4194304 | tf_op jit(solution)/shard_map/all_to_all | solution.py:9
  299.6 34.6 %copy-start.3 = (f32[64,8]{0,1:T(8,128)S(1)}, f32[64,8]{0,1:T(8,128)}, u32[]{:S(2)}) copy-start(f32[64,8]{0,1:T(8,128)} %param.11) | copy-start | bytes 6148
  317.0 1.3 copy-start.1
  318.4 158.8 %all-to-all-start.3 = ((bf16[32,24,1792]{2,1,0:T(8,128)(2,1)}), bf16[32,24,1792]{2,1,0:T(8,128)(2,1)S(1)}, u32[]{:S(2)}, u32[]{:S(2)}) async-start(bf16[32,24,1792]{2,1,0:T(8,128)(2,1)} %bitcast.57), calls=%async_computation.4 | async-start | bytes 5505024 | tf_op jit(solution)/shard_map/all_to_all | solution.py:82
  333.3 150.2 %all-gather.8.cloned.1.call-start = ((), (), s32[]{:S(2)}) async-start(), calls=%async_computation.7 | async-start | bytes 3784704 | tf_op jit(solution)/shard_map/all_gather | solution.py:103
Sparse Core Ops, SparseCore 0:
  10.1 143.7 all-gather.3
  155.7 85.5 all-gather.5
  336.0 129.1 all-gather.7
Sparse Core Ops, SparseCore 1:
  192.7 66.9 reduce-scatter.1
where the time goes:
time: 495 us; the launch traced here: 494 us
  waiting for transfers between devices  378 us (76%)
  starting transfers between devices  48.1 us (10%)
  matrix products  27.7 us (6%)
  between operations  14.8 us (3%)
  other arithmetic  13.2 us (3%)
  local copies, waits for them, and re-layouts  12.7 us (3%)
    all_to_all x1, waiting for transfers between devices, per_device(): lax.all_to_all(outgoing, 'ep', split_axis=0, concat_axis=0, tiled=True)  141 us
    all_to_all x1, waiting for transfers between devices, per_device(): lax.all_to_all(expert_out, 'ep', split_axis=0, concat_axis=0, tiled=True)  137 us
    all_gather x1, waiting for transfers between devices, per_device(): lax.all_gather(shared_up, 'ep', axis=0, tiled=True)  45.4 us
    all_to_all x2, waiting for transfers between devices, from_everyone(): return lax.all_to_all(copies, axis, split_axis=0, concat_axis=0, tiled=True)  37.3 us
    all_to_all x1, starting transfers between devices, per_device(): lax.all_to_all(outgoing, 'ep', split_axis=0, concat_axis=0, tiled=True)  25.5 us
    reduce_scatter x1, waiting for transfers between devices, per_device(): lax.psum_scatter(jnp.concatenate([gate_part, up_part], axis=1), 'sub', sc...  15 us
    all_to_all x1, starting transfers between devices, per_device(): lax.all_to_all(expert_out, 'ep', split_axis=0, concat_axis=0, tiled=True)  14.9 us
  transfers between devices with their start and end apart: 8, of which 6 were waited for; matrix products, arithmetic and copies ran while one was open for 9% of the time, Pallas kernels for 0%

commit v1 on v0

v1 whole, which is shorter than its diff:
```python
import functools

import jax
import jax.numpy as jnp
from jax import lax
from jax.experimental import pallas as pl
from jax.experimental.pallas import tpu as pltpu
from jax.sharding import PartitionSpec as P

MESH = pl.DeviceIdType.MESH
NC = 4


def layer_kernel(
    dims,
    tokens_ref,
    meta_ref,
    sgate_ref,
    sup_ref,
    sdown_ref,
    gate_hbm,
    up_hbm,
    down_hbm,
    out_ref,
    gate_v,
    up_v,
    down_v,
    tok,
    meta,
    comp,
    upper,
    lhs_t,
    wsel,
    xs,
    xr1,
    xc,
    xr2,
    ss,
    sr1,
    sc,
    sr2,
    hid,
    hsb,
    con,
    ps,
    pr,
    rs_s,
    rs_r,
    w_sem,
    ag_ss,
    ag_rs,
    dd_ss,
    dd_rs,
    x1_ss,
    x1_rs,
    x2_ss,
    x2_rs,
    h1_ss,
    h1_rs,
    h2_ss,
    h2_rs,
    pd_ss,
    pd_rs,
    r_ss,
    r_rs,
):
    nz, nsub, cap, units = dims
    f32, bf16 = jnp.float32, jnp.bfloat16
    H = nz // 2
    T, Q = tokens_ref.shape
    CH = T // NC
    R = 4 * cap
    HQ = gate_v.shape[1] // nsub
    UQ = units // nsub
    TILE = 256
    ntile = Q // TILE

    e = lax.axis_index("ep")
    s = lax.axis_index("sub")
    z = e // 2
    c = e % 2
    z_right = {"ep": ((z + 1) % nz) * 2 + c}
    z_left = {"ep": ((z + nz - 1) % nz) * 2 + c}
    z_next = (z_right, z_left)
    partner = {"ep": z * 2 + (1 - c)}
    xR = (s + 1) % nsub
    xL = (s + nsub - 1) % nsub
    xO = (s + 2) % nsub
    x_right = {"sub": xR}
    x_left = {"sub": xL}

    def remote(src, dst, ssem, rsem, dev):
        return pltpu.make_async_remote_copy(
            src_ref=src, dst_ref=dst, send_sem=ssem, recv_sem=rsem, device_id=dev, device_id_type=MESH
        )

    weights = [
        pltpu.make_async_copy(a, b, w_sem.at[n])
        for n, (a, b) in enumerate(((gate_hbm, gate_v), (up_hbm, up_v), (down_hbm, down_v)))
    ]
    for w in weights:
        w.start()

    barrier = pltpu.get_barrier_semaphore()
    for peer in (z_right, z_left, partner, x_right, x_left):
        pl.semaphore_signal(barrier, inc=1, device_id=peer, device_id_type=MESH)
    pl.semaphore_wait(barrier, 5)

    def mine(m, i):
        return (i < NC // 2 or i == NC) if m == 0 else (NC // 2 <= i < NC)

    def slot_of(m, t):
        return m * (1 - t // H)

    def rows_of(d, rel, i):
        return pl.ds((2 * d + rel) * T + i * CH, CH)

    def ring(m, t, i, first=False):
        d = slot_of(m, t)
        if i == NC:
            src = meta_ref if first else meta.at[t - 2, 2 * m]
            dst = meta.at[t - 1, 2 * d]
        else:
            src = tokens_ref.at[pl.ds(i * CH, CH)] if first else tok.at[t - 2, rows_of(m, 0, i)]
            dst = tok.at[t - 1, rows_of(d, 0, i)]
        return remote(src, dst, ag_ss.at[m, t - 1, i], ag_rs.at[m, t - 1, i], z_next[m])

    def ring_arrival(m, t, i):
        d = slot_of(m, t)
        dst = meta.at[t - 1, 2 * d] if i == NC else tok.at[t - 1, rows_of(d, 0, i)]
        return remote(dst, dst, ag_ss.at[m, t - 1, i], ag_rs.at[m, t - 1, i], z_next[m])

    def hand(d, t, i, own=False):
        if i == NC:
            src = meta_ref if own else meta.at[t - 1, 2 * d]
            dst = meta.at[t - 1, 2 * d + 1]
        else:
            src = tokens_ref.at[pl.ds(i * CH, CH)] if own else tok.at[t - 1, rows_of(d, 0, i)]
            dst = tok.at[t - 1, rows_of(d, 1, i)]
        return remote(src, dst, dd_ss.at[d, t - 1, i], dd_rs.at[d, t - 1, i], partner)

    order = [0, NC] + list(range(1, NC))
    for i in order:
        for m in (0, 1):
            if H > 1 or mine(m, i):
                ring(m, 1, i, first=True).start()
    for i in order:
        hand(1, H, i, own=True).start()
    tok[H - 1, 2 * T : 3 * T, :] = tokens_ref[...]
    meta[H - 1, 2] = meta_ref[...]

    row_i = lax.broadcasted_iota(jnp.int32, (4 * T, 4 * T), 0)
    col_i = lax.broadcasted_iota(jnp.int32, (4 * T, 4 * T), 1)
    upper[...] = ((row_i < col_i) & (row_i // T == col_i // T)).astype(f32).astype(bf16)

    def forward(t, i):
        for m in (0, 1):

            @pl.when(t < H)
            def _():
                ring_arrival(m, t, i).wait_recv()
                if mine(m, i):
                    ring(m, t + 1, i).start()
                else:

                    @pl.when(t + 1 < H)
                    def _():
                        ring(m, t + 1, i).start()

                hand(m, t, i).start()

            if mine(m, i):

                @pl.when(t == H)
                def _():
                    ring_arrival(m, t, i).wait_recv()
                    hand(0, t, i).start()

    def stage1a(k):
        for d in (0, 1):
            for i in range(NC + 1):
                hand(d, k, i).wait_recv()
        half = lax.broadcasted_iota(jnp.int32, meta_ref.shape, 1) < T
        ids, ws = [], []
        for d in (0, 1):
            m0 = meta[k - 1, 2 * d]
            m1 = meta[k - 1, 2 * d + 1]
            ids.append(jnp.where(half, m0, pltpu.roll(m1, T, 1)))
            ws.append(jnp.where(half, pltpu.roll(m0, T, 1), m1))
        ids = jnp.concatenate(ids, axis=1)
        ws = jnp.concatenate(ws, axis=1)
        hit = ids == e.astype(f32)
        sel = jnp.max(jnp.where(hit, 1.0, 0.0), axis=0, keepdims=True)
        wsel[k - 1] = jnp.broadcast_to(
            jnp.sum(jnp.where(hit, ws, 0.0), axis=0, keepdims=True), (8, 4 * T)
        )
        sel8 = jnp.broadcast_to(sel, (16, 4 * T)).astype(bf16)
        pos = jnp.dot(sel8, upper[...], preferred_element_type=f32)[0:1]
        base = (lax.broadcasted_iota(jnp.int32, (1, 4 * T), 1) // T * cap).astype(f32)
        target = jnp.where(sel > 0.0, pos + base, -1.0)
        place = lax.broadcasted_iota(jnp.int32, (R, 4 * T), 0).astype(f32) == target
        place = jnp.where(place, 1.0, 0.0).astype(bf16)
        lhs_t[k - 1, 0:R, :] = place

        def pick(n, _):
            cols = pl.ds(pl.multiple_of(n * TILE, TILE), TILE)
            comp[:, cols] = jnp.dot(place, tok[k - 1, :, cols], preferred_element_type=f32).astype(bf16)
            return 0

        lax.fori_loop(0, ntile, pick, 0)

    def x_first(k):
        return (
            remote(xs.at[k - 1, xO, 0], xr1.at[k - 1, 0], x1_ss.at[k - 1, 0], x1_rs.at[k - 1, 0], x_right),
            remote(xs.at[k - 1, xO, 1], xr1.at[k - 1, 2], x1_ss.at[k - 1, 2], x1_rs.at[k - 1, 2], x_left),
            remote(ss.at[k - 1, xO, 0], sr1.at[k - 1, 0], x1_ss.at[k - 1, 4], x1_rs.at[k - 1, 4], x_right),
            remote(ss.at[k - 1, xO, 1], sr1.at[k - 1, 2], x1_ss.at[k - 1, 6], x1_rs.at[k - 1, 6], x_left),
            remote(xs.at[k - 1, xR, 1], xr1.at[k - 1, 1], x1_ss.at[k - 1, 1], x1_rs.at[k - 1, 1], x_right),
            remote(xs.at[k - 1, xL, 0], xr1.at[k - 1, 3], x1_ss.at[k - 1, 3], x1_rs.at[k - 1, 3], x_left),
            remote(ss.at[k - 1, xR, 1], sr1.at[k - 1, 1], x1_ss.at[k - 1, 5], x1_rs.at[k - 1, 5], x_right),
            remote(ss.at[k - 1, xL, 0], sr1.at[k - 1, 3], x1_ss.at[k - 1, 7], x1_rs.at[k - 1, 7], x_left),
        )

    def stage1b(k):
        rows = comp[...]

        def project(j, _):
            cols = pl.ds(pl.multiple_of(j * HQ, HQ), HQ)
            xs[k - 1, j, 0] = jnp.dot(rows, gate_v[:, cols], preferred_element_type=f32).astype(bf16)
            xs[k - 1, j, 1] = jnp.dot(rows, up_v[:, cols], preferred_element_type=f32).astype(bf16)
            return 0

        lax.fori_loop(0, nsub, project, 0)
        contract = (((1,), (1,)), ((), ()))
        pre = lax.dot_general(sgate_ref[...], tok[k - 1], contract, preferred_element_type=f32)
        lin = lax.dot_general(sup_ref[...], tok[k - 1], contract, preferred_element_type=f32)
        for j in range(nsub):
            ss[k - 1, j, 0] = pre[j * UQ : (j + 1) * UQ]
            ss[k - 1, j, 1] = lin[j * UQ : (j + 1) * UQ]
        for copy in x_first(k):
            copy.start()

    def x_second(k):
        return (
            remote(xc.at[k - 1, 0], xr2.at[k - 1, 0], x2_ss.at[k - 1, 0], x2_rs.at[k - 1, 0], x_right),
            remote(xc.at[k - 1, 1], xr2.at[k - 1, 1], x2_ss.at[k - 1, 1], x2_rs.at[k - 1, 1], x_left),
            remote(sc.at[k - 1, 0], sr2.at[k - 1, 0], x2_ss.at[k - 1, 2], x2_rs.at[k - 1, 2], x_right),
            remote(sc.at[k - 1, 1], sr2.at[k - 1, 1], x2_ss.at[k - 1, 3], x2_rs.at[k - 1, 3], x_left),
        )

    def stage2(k):
        first = x_first(k)
        second = x_second(k)
        for m, toward in ((0, xR), (1, xL)):
            first[m].wait_recv()
            xc[k - 1, m] = (
                xs[k - 1, toward, m].astype(f32) + xr1[k - 1, 2 * m].astype(f32)
            ).astype(bf16)
            second[m].start()
        for m, toward in ((0, xR), (1, xL)):
            first[2 + m].wait_recv()
            sc[k - 1, m] = ss[k - 1, toward, m] + sr1[k - 1, 2 * m]
            second[2 + m].start()

    own_cols = pl.ds(pl.multiple_of(s * HQ, HQ), HQ)
    left_cols = pl.ds(pl.multiple_of(xL * HQ, HQ), HQ)
    right_cols = pl.ds(pl.multiple_of(xR * HQ, HQ), HQ)
    far_cols = pl.ds(pl.multiple_of(xO * HQ, HQ), HQ)
    own_rows = pl.ds(pl.multiple_of(s * UQ, UQ), UQ)
    left_rows = pl.ds(pl.multiple_of(xL * UQ, UQ), UQ)
    right_rows = pl.ds(pl.multiple_of(xR * UQ, UQ), UQ)
    far_rows = pl.ds(pl.multiple_of(xO * UQ, UQ), UQ)

    def h_copy(k, n, cols, rows, dev):
        view = hid.at[k - 1, :, cols]
        small = hsb.at[k - 1, rows, :]
        return (
            remote(view, view, h1_ss.at[k - 1, n], h1_rs.at[k - 1, n], dev),
            remote(small, small, h1_ss.at[k - 1, 2 + n], h1_rs.at[k - 1, 2 + n], dev),
        )

    def stage3(k):
        for copy in x_first(k)[4:]:
            copy.wait_recv()
        for copy in x_second(k):
            copy.wait_recv()
        gate = xs[k - 1, s, 0].astype(f32) + xr1[k - 1, 3].astype(f32) + xr2[k - 1, 0].astype(f32)
        up = xs[k - 1, s, 1].astype(f32) + xr1[k - 1, 1].astype(f32) + xr2[k - 1, 1].astype(f32)
        hid[k - 1, :, own_cols] = (gate / (1.0 + jnp.exp(-gate)) * up).astype(bf16)
        sg = ss[k - 1, s, 0] + sr1[k - 1, 3] + sr2[k - 1, 0]
        su = ss[k - 1, s, 1] + sr1[k - 1, 1] + sr2[k - 1, 1]
        hsb[k - 1, own_rows, :] = sg / (1.0 + jnp.exp(-sg)) * su
        for copy in h_copy(k, 0, own_cols, own_rows, x_right) + h_copy(k, 1, own_cols, own_rows, x_left):
            copy.start()

    def h_far(k, n, cols, rows, dev):
        view = hid.at[k - 1, pl.ds(n * (R // 2), R // 2), cols]
        small = hsb.at[k - 1, rows, pl.ds(n * 2 * T, 2 * T)]
        return (
            remote(view, view, h2_ss.at[k - 1, n], h2_rs.at[k - 1, n], dev),
            remote(small, small, h2_ss.at[k - 1, 2 + n], h2_rs.at[k - 1, 2 + n], dev),
        )

    def stage4(k):
        for n, cols, rows, dev in ((0, left_cols, left_rows, x_right), (1, right_cols, right_rows, x_left)):
            for copy in h_copy(k, n, cols, rows, dev):
                copy.wait_recv()
            for copy in h_far(k, n, cols, rows, dev):
                copy.start()

    def give(k, d):
        return remote(ps.at[k - 1, d], pr.at[k - 1, d], pd_ss.at[k - 1, d], pd_rs.at[k - 1, d], partner)

    def stage5(k):
        for n, dev in ((0, x_right), (1, x_left)):
            for copy in h_far(k, n, far_cols, far_rows, dev):
                copy.wait_recv()
        lhs_t[k - 1, R : R + units, :] = hsb[k - 1].astype(bf16)
        both_t = lhs_t[k - 1]
        weight = jnp.sum(both_t[0:R].astype(f32) * wsel[k - 1, 0:1], axis=1, keepdims=True)
        both = jnp.transpose(both_t.astype(f32)).astype(bf16)
        hidden = hid[k - 1]

        def columns(n, _):
            cols = pl.ds(pl.multiple_of(n * TILE, TILE), TILE)
            o = jnp.dot(hidden, down_v[:, cols], preferred_element_type=f32)
            o = (o * weight).astype(bf16)
            stacked = jnp.concatenate([o, sdown_ref[:, cols]], axis=0)
            part = jnp.dot(both, stacked, preferred_element_type=f32)
            for d in (0, 1):
                con[k - 1, d, :, cols] = part[2 * d * T : (2 * d + 1) * T]
                ps[k - 1, d, :, cols] = part[(2 * d + 1) * T : (2 * d + 2) * T].astype(bf16)
            return 0

        lax.fori_loop(0, ntile, columns, 0)
        for d in (0, 1):
            give(k, d).start()

    def during(k, stage):
        @pl.when((k >= 1) & (k <= H))
        def _():
            stage(k)

    def step(t, _):
        forward(t, 0)
        forward(t, NC)

        @pl.when(t == 2)
        def _():
            for w in weights:
                w.wait()

        during(t - 1, stage1a)
        forward(t, 1)
        during(t - 1, stage1b)
        forward(t, 2)
        during(t - 5, stage5)
        forward(t, 3)
        during(t - 4, stage4)
        during(t - 3, stage3)
        during(t - 2, stage2)
        return 0

    lax.fori_loop(1, H + 6, step, 0)

    def rows(i):
        return pl.ds(i * CH, CH)

    def pass_on(m, d, i):
        return remote(
            rs_s.at[m, d - 1, rows(i)],
            rs_r.at[m, d - 1, rows(i)],
            r_ss.at[m, d - 1, i],
            r_rs.at[m, d - 1, i],
            z_next[m],
        )

    def own_sum(d, slot, i):
        return con[d - 1, slot, rows(i), :] + pr[d - 1, slot, rows(i), :].astype(f32)

    give(H, 0).wait_recv()
    for i in range(NC):
        m = 0 if mine(0, i) else 1
        rs_s[m, H - 1, rows(i), :] = own_sum(H, 0, i).astype(bf16)
        pass_on(m, H, i).start()

    def back(d, partly):
        give(d, 0).wait_recv()
        give(d, 1).wait_recv()
        for i in range(NC):
            for m in (0, 1):
                total = own_sum(d, 1 - m, i)
                if not partly or mine(m, i):
                    pass_on(m, d + 1, i).wait_recv()
                    total = total + rs_r[m, d, rows(i), :].astype(f32)
                rs_s[m, d - 1, rows(i), :] = total.astype(bf16)
                pass_on(m, d, i).start()

    if H > 1:
        back(H - 1, True)

    def back_step(n, _):
        back(H - 2 - n, False)
        return 0

    lax.fori_loop(0, H - 2, back_step, 0)
    give(H, 1).wait_recv()
    for i in range(NC):
        total = own_sum(H, 1, i)
        for m in (0, 1):
            pass_on(m, 1, i).wait_recv()
            total = total + rs_r[m, 0, rows(i), :].astype(f32)
        out_ref[rows(i), :] = total.astype(bf16)

    def drain(k, _):
        for i in range(NC + 1):
            for m in (0, 1):
                hand(m, k, i).wait_send()

                @pl.when(k < H)
                def _():
                    ring_arrival(m, k, i).wait_send()

                if mine(m, i):

                    @pl.when(k == H)
                    def _():
                        ring_arrival(m, k, i).wait_send()

        for copy in x_first(k) + x_second(k):
            copy.wait_send()
        for n, dev in ((0, x_right), (1, x_left)):
            for copy in h_copy(k, n, own_cols, own_rows, dev) + h_far(k, n, own_cols, own_rows, dev):
                copy.wait_send()
            give(k, n).wait_send()
        for i in range(NC):
            for m in (0, 1):

                @pl.when(k < H)
                def _():
                    pass_on(m, k, i).wait_send()

                if mine(m, i):

                    @pl.when(k == H)
                    def _():
                        pass_on(m, k, i).wait_send()

        return 0

    lax.fori_loop(1, H + 1, drain, 0)


def per_device(
    tokens,
    expert_ids,
    route_weights,
    gate_weight,
    up_weight,
    down_weight,
    shared_gate,
    shared_up,
    shared_down,
):
    f32, bf16 = jnp.float32, jnp.bfloat16
    nep = lax.axis_size("ep")
    nsub = lax.axis_size("sub")
    nz = nep // 2
    H = nz // 2
    T, Q = tokens.shape
    top = expert_ids.shape[1]
    cap = T * top * 3 // (2 * nep)
    units = shared_gate.shape[0]
    hidden = gate_weight.shape[2]
    HQ, UQ, R = hidden // nsub, units // nsub, 4 * cap
    meta = jnp.concatenate([expert_ids.T.astype(f32), route_weights.T], axis=1)
    vmem = pltpu.VMEM
    dma = pltpu.SemaphoreType.DMA
    vspec = pl.BlockSpec(memory_space=pltpu.VMEM)
    hspec = pl.BlockSpec(memory_space=pl.ANY)
    scratch = [
        vmem((Q, hidden), bf16),
        vmem((Q, hidden), bf16),
        vmem((hidden, Q), bf16),
        vmem((H, 4 * T, Q), bf16),
        vmem((H, 4, top, 2 * T), f32),
        vmem((R, Q), bf16),
        vmem((4 * T, 4 * T), bf16),
        vmem((H, R + units, 4 * T), bf16),
        vmem((H, 8, 4 * T), f32),
        vmem((H, nsub, 2, R, HQ), bf16),
        vmem((H, 4, R, HQ), bf16),
        vmem((H, 2, R, HQ), bf16),
        vmem((H, 2, R, HQ), bf16),
        vmem((H, nsub, 2, UQ, 4 * T), f32),
        vmem((H, 4, UQ, 4 * T), f32),
        vmem((H, 2, UQ, 4 * T), f32),
        vmem((H, 2, UQ, 4 * T), f32),
        vmem((H, R, hidden), bf16),
        vmem((H, units, 4 * T), f32),
        vmem((H, 2, T, Q), f32),
        vmem((H, 2, T, Q), bf16),
        vmem((H, 2, T, Q), bf16),
        vmem((2, H, T, Q), bf16),
        vmem((2, H, T, Q), bf16),
        dma((3,)),
    ]
    for shape in ((2, H, NC + 1), (2, H, NC + 1), (H, 8), (H, 4), (H, 4), (H, 4), (H, 2), (2, H, NC)):
        scratch += [dma(shape), dma(shape)]
    return pl.pallas_call(
        functools.partial(layer_kernel, (nz, nsub, cap, units)),
        out_shape=jax.ShapeDtypeStruct((T, Q), bf16),
        in_specs=[vspec] * 5 + [hspec] * 3,
        out_specs=vspec,
        scratch_shapes=scratch,
        compiler_params=pltpu.CompilerParams(
            collective_id=0, has_side_effects=True, vmem_limit_bytes=67043328
        ),
    )(
        tokens,
        meta,
        shared_gate,
        shared_up,
        shared_down,
        gate_weight[0],
        up_weight[0],
        down_weight[0],
    )


def solution(mesh):
    in_specs = (
        P(("groups", "ep"), "sub"),
        P(("groups", "ep"), None),
        P(("groups", "ep"), None),
        P("ep", "sub", None),
        P("ep", "sub", None),
        P("ep", None, "sub"),
        P("ep", "sub"),
        P("ep", "sub"),
        P("ep", "sub"),
    )
    out_specs = P(("groups", "ep"), "sub")
    return jax.shard_map(
        per_device, mesh=mesh, in_specs=in_specs, out_specs=out_specs, check_vma=False
    )
```

time: 495 us -> 171 us (0.35)
  waiting for transfers between devices: 378 us -> 0 us
  Pallas kernels: 0 us -> 167 us
  starting transfers between devices: 48.1 us -> 0 us
  matrix products: 27.7 us -> 0 us
  between operations: 14.8 us -> 0.01 us
  other arithmetic: 13.2 us -> 2.04 us
  local copies, waits for them, and re-layouts: 12.7 us -> 1.64 us
    all_to_all x4 -> x0, waiting for transfers between devices: 315 us -> none  [the longest x1 141 us: per_device(): lax.all_to_all(outgoing, 'ep', split_axis=0, concat_axis=0, tiled=True)]
    pallas_call x0 -> x1, Pallas kernels: none -> 167 us  [per_device(): pl.pallas_call(functools.partial(layer_kernel, (nz, nsub, cap, units)), o...]
    all_to_all x4 -> x0, starting transfers between devices: 47.9 us -> none  [the longest x1 25.5 us: per_device(): lax.all_to_all(outgoing, 'ep', split_axis=0, concat_axis=0, tiled=True)]
    all_gather x3 -> x0, waiting for transfers between devices: 45.4 us -> none  [the longest x1 45.4 us: per_device(): lax.all_gather(shared_up, 'ep', axis=0, tiled=True)]
    dot_general x7 -> x0, matrix products: 27.7 us -> none  [the longest x1 7.05 us: per_device(): jnp.dot(expert_hidden, down_weight[0], preferred_element_type=jnp.float32)]
    reduce_scatter x1 -> x0, waiting for transfers between devices: 15 us -> none  [per_device(): lax.psum_scatter(jnp.concatenate([gate_part, up_part], axis=1), 'sub', sc...]
    reduce_sum x3 -> x0, other arithmetic: 6.73 us -> none  [the longest x1 3.52 us: of_everyone(): return from_everyone(value, axis).sum(axis=0)]
  transfers between devices with their start and end apart: 8 -> 0, of which waited for: 6 -> 0; matrix products, arithmetic and copies ran while one was open for 9% -> 0% of each run, Pallas kernels for 0% -> 0%
where the time goes in v1:
time: 171 us
  Pallas kernels  167 us (98%)
  other arithmetic  2.04 us (1%)
    pallas_call x1, Pallas kernels, per_device(): pl.pallas_call(functools.partial(layer_kernel, (nz, nsub, cap, units)), o...  167 us

profile of v1, /device:TPU:33, one launch (start us, length us, event | category | flops | bytes accessed | tf_op | source)
XLA Modules:
  0.0 170.9 jit_solution(2729635833570460518)
XLA Ops:
  0.0 0.7 convert_bitcast_fusion
  0.7 1.4 pad_maximum_fusion.meta_ref
  2.0 167.2 %shard_map.91 = bf16[64,1792]{1,0:T(8,128)(2,1)} custom-call(bf16[64,1792]{1,0:T(8,128)(2,1)} %tokens_ref.1, f32[8,128]{1,0:T(8,128)} %pad_maximum_fusion.meta_ref, bf16[32,1792]{1,0:T(8,128)(2,1)} %sgate_ref.1, bf16[32,1792]{1,0:T(8,128)(2,1)} %sup_ref.1, bf16[32,1792]{1,0:T(8,128)(2,1)} %sdown_ref.1, bf16[1792,1024]{1,0:T(8,128)(2,1)} %bitcast.6, ...), custom_call_target="tpu_custom_call" | custom-call | tf_op jit(solution)/shard_map/pallas_call | solution.py:510
  169.2 1.6 copy.11

commit v2 on v1

--- a/solution.py
+++ b/solution.py
@@ -13,15 +13,19 @@
 
 def layer_kernel(
     dims,
-    tokens_ref,
-    meta_ref,
-    sgate_ref,
-    sup_ref,
-    sdown_ref,
+    ids_ref,
+    route_ref,
+    tokens_hbm,
+    sgate_hbm,
+    sup_hbm,
+    sdown_hbm,
     gate_hbm,
     up_hbm,
     down_hbm,
     out_ref,
+    sgate_ref,
+    sup_ref,
+    sdown_ref,
     gate_v,
     up_v,
     down_v,
@@ -67,7 +71,7 @@
     nz, nsub, cap, units = dims
     f32, bf16 = jnp.float32, jnp.bfloat16
     H = nz // 2
-    T, Q = tokens_ref.shape
+    T, Q = tokens_hbm.shape
     CH = T // NC
     R = 4 * cap
     HQ = gate_v.shape[1] // nsub
@@ -96,15 +100,29 @@
 
     weights = [
         pltpu.make_async_copy(a, b, w_sem.at[n])
-        for n, (a, b) in enumerate(((gate_hbm, gate_v), (up_hbm, up_v), (down_hbm, down_v)))
+        for n, (a, b) in enumerate(
+            (
+                (gate_hbm, gate_v),
+                (up_hbm, up_v),
+                (sgate_hbm, sgate_ref),
+                (sup_hbm, sup_ref),
+                (sdown_hbm, sdown_ref),
+                (down_hbm, down_v),
+            )
+        )
     ]
-    for w in weights:
-        w.start()
+    own_tokens = tok.at[H - 1, pl.ds(2 * T, T)]
+    own_meta = meta.at[H - 1, 2]
+    fetch = pltpu.make_async_copy(tokens_hbm, own_tokens, w_sem.at[6])
+    fetch.start()
+    own_meta[:, 0:T] = ids_ref[...].astype(f32)
+    own_meta[:, T : 2 * T] = route_ref[...]
 
     barrier = pltpu.get_barrier_semaphore()
     for peer in (z_right, z_left, partner, x_right, x_left):
         pl.semaphore_signal(barrier, inc=1, device_id=peer, device_id_type=MESH)
     pl.semaphore_wait(barrier, 5)
+    fetch.wait()
 
     def mine(m, i):
         return (i < NC // 2 or i == NC) if m == 0 else (NC // 2 <= i < NC)
@@ -118,10 +136,10 @@
     def ring(m, t, i, first=False):
         d = slot_of(m, t)
         if i == NC:
-            src = meta_ref if first else meta.at[t - 2, 2 * m]
+            src = own_meta if first else meta.at[t - 2, 2 * m]
             dst = meta.at[t - 1, 2 * d]
         else:
-            src = tokens_ref.at[pl.ds(i * CH, CH)] if first else tok.at[t - 2, rows_of(m, 0, i)]
+            src = own_tokens.at[pl.ds(i * CH, CH)] if first else tok.at[t - 2, rows_of(m, 0, i)]
             dst = tok.at[t - 1, rows_of(d, 0, i)]
         return remote(src, dst, ag_ss.at[m, t - 1, i], ag_rs.at[m, t - 1, i], z_next[m])
 
@@ -132,10 +150,10 @@
 
     def hand(d, t, i, own=False):
         if i == NC:
-            src = meta_ref if own else meta.at[t - 1, 2 * d]
+            src = own_meta if own else meta.at[t - 1, 2 * d]
             dst = meta.at[t - 1, 2 * d + 1]
         else:
-            src = tokens_ref.at[pl.ds(i * CH, CH)] if own else tok.at[t - 1, rows_of(d, 0, i)]
+            src = own_tokens.at[pl.ds(i * CH, CH)] if own else tok.at[t - 1, rows_of(d, 0, i)]
             dst = tok.at[t - 1, rows_of(d, 1, i)]
         return remote(src, dst, dd_ss.at[d, t - 1, i], dd_rs.at[d, t - 1, i], partner)
 
@@ -146,8 +164,8 @@
                 ring(m, 1, i, first=True).start()
     for i in order:
         hand(1, H, i, own=True).start()
-    tok[H - 1, 2 * T : 3 * T, :] = tokens_ref[...]
-    meta[H - 1, 2] = meta_ref[...]
+    for w in weights:
+        w.start()
 
     row_i = lax.broadcasted_iota(jnp.int32, (4 * T, 4 * T), 0)
     col_i = lax.broadcasted_iota(jnp.int32, (4 * T, 4 * T), 1)
@@ -180,7 +198,7 @@
         for d in (0, 1):
             for i in range(NC + 1):
                 hand(d, k, i).wait_recv()
-        half = lax.broadcasted_iota(jnp.int32, meta_ref.shape, 1) < T
+        half = lax.broadcasted_iota(jnp.int32, own_meta.shape, 1) < T
         ids, ws = [], []
         for d in (0, 1):
             m0 = meta[k - 1, 2 * d]
@@ -202,12 +220,7 @@
         place = jnp.where(place, 1.0, 0.0).astype(bf16)
         lhs_t[k - 1, 0:R, :] = place
 
-        def pick(n, _):
-            cols = pl.ds(pl.multiple_of(n * TILE, TILE), TILE)
-            comp[:, cols] = jnp.dot(place, tok[k - 1, :, cols], preferred_element_type=f32).astype(bf16)
-            return 0
-
-        lax.fori_loop(0, ntile, pick, 0)
+        comp[...] = jnp.dot(place, tok[k - 1], preferred_element_type=f32).astype(bf16)
 
     def x_first(k):
         return (
@@ -224,13 +237,11 @@
     def stage1b(k):
         rows = comp[...]
 
-        def project(j, _):
-            cols = pl.ds(pl.multiple_of(j * HQ, HQ), HQ)
-            xs[k - 1, j, 0] = jnp.dot(rows, gate_v[:, cols], preferred_element_type=f32).astype(bf16)
-            xs[k - 1, j, 1] = jnp.dot(rows, up_v[:, cols], preferred_element_type=f32).astype(bf16)
-            return 0
-
-        lax.fori_loop(0, nsub, project, 0)
+        ga = jnp.dot(rows, gate_v[...], preferred_element_type=f32).astype(bf16)
+        ua = jnp.dot(rows, up_v[...], preferred_element_type=f32).astype(bf16)
+        for j in range(nsub):
+            xs[k - 1, j, 0] = ga[:, j * HQ : (j + 1) * HQ]
+            xs[k - 1, j, 1] = ua[:, j * HQ : (j + 1) * HQ]
         contract = (((1,), (1,)), ((), ()))
         pre = lax.dot_general(sgate_ref[...], tok[k - 1], contract, preferred_element_type=f32)
         lin = lax.dot_general(sup_ref[...], tok[k - 1], contract, preferred_element_type=f32)
@@ -321,18 +332,13 @@
         both = jnp.transpose(both_t.astype(f32)).astype(bf16)
         hidden = hid[k - 1]
 
-        def columns(n, _):
-            cols = pl.ds(pl.multiple_of(n * TILE, TILE), TILE)
-            o = jnp.dot(hidden, down_v[:, cols], preferred_element_type=f32)
-            o = (o * weight).astype(bf16)
-            stacked = jnp.concatenate([o, sdown_ref[:, cols]], axis=0)
-            part = jnp.dot(both, stacked, preferred_element_type=f32)
-            for d in (0, 1):
-                con[k - 1, d, :, cols] = part[2 * d * T : (2 * d + 1) * T]
-                ps[k - 1, d, :, cols] = part[(2 * d + 1) * T : (2 * d + 2) * T].astype(bf16)
-            return 0
-
-        lax.fori_loop(0, ntile, columns, 0)
+        o = jnp.dot(hidden, down_v[...], preferred_element_type=f32)
+        o = (o * weight).astype(bf16)
+        stacked = jnp.concatenate([o, sdown_ref[...]], axis=0)
+        part = jnp.dot(both, stacked, preferred_element_type=f32)
+        for d in (0, 1):
+            con[k - 1, d] = part[2 * d * T : (2 * d + 1) * T]
+            ps[k - 1, d] = part[(2 * d + 1) * T : (2 * d + 2) * T].astype(bf16)
         for d in (0, 1):
             give(k, d).start()
 
@@ -473,12 +479,11 @@
     units = shared_gate.shape[0]
     hidden = gate_weight.shape[2]
     HQ, UQ, R = hidden // nsub, units // nsub, 4 * cap
-    meta = jnp.concatenate([expert_ids.T.astype(f32), route_weights.T], axis=1)
     vmem = pltpu.VMEM
     dma = pltpu.SemaphoreType.DMA
     vspec = pl.BlockSpec(memory_space=pltpu.VMEM)
     hspec = pl.BlockSpec(memory_space=pl.ANY)
-    scratch = [
+    scratch = [vmem((units, Q), bf16)] * 3 + [
         vmem((Q, hidden), bf16),
         vmem((Q, hidden), bf16),
         vmem((hidden, Q), bf16),
@@ -503,22 +508,23 @@
         vmem((H, 2, T, Q), bf16),
         vmem((2, H, T, Q), bf16),
         vmem((2, H, T, Q), bf16),
-        dma((3,)),
+        dma((7,)),
     ]
     for shape in ((2, H, NC + 1), (2, H, NC + 1), (H, 8), (H, 4), (H, 4), (H, 4), (H, 2), (2, H, NC)):
         scratch += [dma(shape), dma(shape)]
     return pl.pallas_call(
         functools.partial(layer_kernel, (nz, nsub, cap, units)),
         out_shape=jax.ShapeDtypeStruct((T, Q), bf16),
-        in_specs=[vspec] * 5 + [hspec] * 3,
+        in_specs=[vspec] * 2 + [hspec] * 7,
         out_specs=vspec,
         scratch_shapes=scratch,
         compiler_params=pltpu.CompilerParams(
             collective_id=0, has_side_effects=True, vmem_limit_bytes=67043328
         ),
     )(
+        expert_ids.T,
+        route_weights.T,
         tokens,
-        meta,
         shared_gate,
         shared_up,
         shared_down,

time: 171 us -> 147 us (0.86)
  Pallas kernels: 167 us -> 145 us
  other arithmetic: 2.04 us -> 0 us
    pallas_call x1, Pallas kernels: 167 us -> 145 us  [per_device(): pl.pallas_call(functools.partial(layer_kernel, (nz, nsub, cap, units)), o...]
where the time goes in v2:
time: 147 us
  Pallas kernels  145 us (99%)
  local copies, waits for them, and re-layouts  1.64 us (1%)
    pallas_call x1, Pallas kernels, per_device(): pl.pallas_call(functools.partial(layer_kernel, (nz, nsub, cap, units)), o...  145 us

profile of v2, /device:TPU:33, one launch (start us, length us, event | category | flops | bytes accessed | tf_op | source)
XLA Modules:
  0.0 147.0 jit_solution(11009582473914193781)
XLA Ops:
  0.0 145.3 %shard_map.91 = bf16[64,1792]{1,0:T(8,128)(2,1)} custom-call(s32[8,64]{1,0:T(8,128)} %bitcast.8, f32[8,64]{1,0:T(8,128)} %bitcast.9, bf16[64,1792]{1,0:T(8,128)(2,1)} %tokens_hbm.1, bf16[32,1792]{1,0:T(8,128)(2,1)} %sgate_hbm.1, bf16[32,1792]{1,0:T(8,128)(2,1)} %sup_hbm.1, bf16[32,1792]{1,0:T(8,128)(2,1)} %sdown_hbm.1, bf16[1792,1024]{1,0:T(8,128)(2,1)} %bitcast.5, ...), custom_call_target="tpu_custom_call" | custom-call | tf_op jit(solution)/shard_map/pallas_call | solution.py:515
  145.3 1.6 %copy.11 = bf16[64,1792]{1,0:T(8,128)(2,1)} copy(bf16[64,1792]{1,0:T(8,128)(2,1)} %shard_map.91) | data formatting | bytes 458752

commit v3 on v2

--- a/solution.py
+++ b/solution.py
@@ -48,11 +48,18 @@
     con,
     ps,
     pr,
+    con_far,
+    ps_home,
+    pr_home,
     rs_s,
     rs_r,
+    fin,
     w_sem,
     ag_ss,
     ag_rs,
+    a1_ss,
+    own_ss,
+    own_rs,
     dd_ss,
     dd_rs,
     x1_ss,
@@ -65,8 +72,11 @@
     h2_rs,
     pd_ss,
     pd_rs,
+    ph_ss,
+    ph_rs,
     r_ss,
     r_rs,
+    f_rs,
 ):
     nz, nsub, cap, units = dims
     f32, bf16 = jnp.float32, jnp.bfloat16
@@ -83,10 +93,15 @@
     s = lax.axis_index("sub")
     z = e // 2
     c = e % 2
-    z_right = {"ep": ((z + 1) % nz) * 2 + c}
-    z_left = {"ep": ((z + nz - 1) % nz) * 2 + c}
-    z_next = (z_right, z_left)
+    ahead = (z + 1 + c * (nz - 2)) % nz
+    behind = (z + nz - 1 + c * 2) % nz
+    z_next = {"ep": ahead * 2 + c}
+    z_prev = {"ep": behind * 2 + c}
+    right_first = {"ep": ((z + 1) % nz) * 2}
+    left_first = {"ep": ((z + nz - 1) % nz) * 2 + 1}
     partner = {"ep": z * 2 + (1 - c)}
+    K = H // 2
+    turn = max(H + 1, K + 5)
     xR = (s + 1) % nsub
     xL = (s + nsub - 1) % nsub
     xO = (s + 2) % nsub
@@ -111,59 +126,85 @@
             )
         )
     ]
-    own_tokens = tok.at[H - 1, pl.ds(2 * T, T)]
-    own_meta = meta.at[H - 1, 2]
+    own_tokens = tok.at[c * K + K - 1, pl.ds(3 * T, T)]
+    own_meta = meta.at[c * K + K - 1, 3]
     fetch = pltpu.make_async_copy(tokens_hbm, own_tokens, w_sem.at[6])
     fetch.start()
     own_meta[:, 0:T] = ids_ref[...].astype(f32)
     own_meta[:, T : 2 * T] = route_ref[...]
 
+    diag_next = {"ep": ahead * 2 + (1 - c)}
+    diag_prev = {"ep": behind * 2 + (1 - c)}
     barrier = pltpu.get_barrier_semaphore()
-    for peer in (z_right, z_left, partner, x_right, x_left):
+    for peer in (z_next, z_prev, diag_next, diag_prev, partner, x_right, x_left):
         pl.semaphore_signal(barrier, inc=1, device_id=peer, device_id_type=MESH)
-    pl.semaphore_wait(barrier, 5)
+    pl.semaphore_wait(barrier, 7)
     fetch.wait()
 
-    def mine(m, i):
-        return (i < NC // 2 or i == NC) if m == 0 else (NC // 2 <= i < NC)
-
-    def slot_of(m, t):
-        return m * (1 - t // H)
-
-    def rows_of(d, rel, i):
-        return pl.ds((2 * d + rel) * T + i * CH, CH)
-
-    def ring(m, t, i, first=False):
-        d = slot_of(m, t)
-        if i == NC:
-            src = own_meta if first else meta.at[t - 2, 2 * m]
-            dst = meta.at[t - 1, 2 * d]
+    def group_of(r, t):
+        return r * K + (t - 1) // 2
+
+    def place_of(t, side):
+        return (t - 1) % 2 * 2 + side
+
+    def block(r, t, side, start=0, size=T):
+        return tok.at[group_of(r, t), pl.ds(pl.multiple_of(place_of(t, side) * T + start, CH), size)]
+
+    def note(r, t, side):
+        return meta.at[group_of(r, t), place_of(t, side)]
+
+    half_rows = T // 2
+
+    def send_first(r):
+        for m, dev in ((0, right_first), (1, left_first)):
+            for i in range(NC + 1):
+                src = own_meta if i == NC else own_tokens.at[pl.ds(i * CH, CH)]
+                dst = note(r, 1, 0) if i == NC else block(r, 1, 0, i * CH, CH)
+                remote(src, dst, a1_ss.at[m, i], ag_rs.at[r, 0, i], dev).start()
+
+    def first_sent(m, i):
+        src = own_meta if i == NC else own_tokens.at[pl.ds(i * CH, CH)]
+        return remote(src, src, a1_ss.at[m, i], ag_rs.at[0, 0, i], z_next)
+
+    def ring(r, t, i):
+        if isinstance(i, int) and i == NC:
+            src, dst = note(r, t - 1, 0), note(r, t, 0)
         else:
-            src = own_tokens.at[pl.ds(i * CH, CH)] if first else tok.at[t - 2, rows_of(m, 0, i)]
-            dst = tok.at[t - 1, rows_of(d, 0, i)]
-        return remote(src, dst, ag_ss.at[m, t - 1, i], ag_rs.at[m, t - 1, i], z_next[m])
-
-    def ring_arrival(m, t, i):
-        d = slot_of(m, t)
-        dst = meta.at[t - 1, 2 * d] if i == NC else tok.at[t - 1, rows_of(d, 0, i)]
-        return remote(dst, dst, ag_ss.at[m, t - 1, i], ag_rs.at[m, t - 1, i], z_next[m])
-
-    def hand(d, t, i, own=False):
-        if i == NC:
-            src = own_meta if own else meta.at[t - 1, 2 * d]
-            dst = meta.at[t - 1, 2 * d + 1]
-        else:
-            src = own_tokens.at[pl.ds(i * CH, CH)] if own else tok.at[t - 1, rows_of(d, 0, i)]
-            dst = tok.at[t - 1, rows_of(d, 1, i)]
-        return remote(src, dst, dd_ss.at[d, t - 1, i], dd_rs.at[d, t - 1, i], partner)
-
-    order = [0, NC] + list(range(1, NC))
-    for i in order:
-        for m in (0, 1):
-            if H > 1 or mine(m, i):
-                ring(m, 1, i, first=True).start()
-    for i in order:
-        hand(1, H, i, own=True).start()
+            src, dst = block(r, t - 1, 0, i * CH, CH), block(r, t, 0, i * CH, CH)
+        return remote(src, dst, ag_ss.at[r, t - 1, i], ag_rs.at[r, t - 1, i], z_next)
+
+    def arrival(r, t, i):
+        dst = note(r, t, 0) if isinstance(i, int) and i == NC else block(r, t, 0, i * CH, CH)
+        return remote(dst, dst, ag_ss.at[r, t - 1, i], ag_rs.at[r, t - 1, i], z_next)
+
+    def hand(r, t):
+        return (
+            remote(block(r, t, 0), block(r, t, 1), dd_ss.at[r, t - 1, 0], dd_rs.at[r, t - 1, 0], partner),
+            remote(note(r, t, 0), note(r, t, 1), dd_ss.at[r, t - 1, 1], dd_rs.at[r, t - 1, 1], partner),
+        )
+
+    def hand_far(r, mine):
+        view = block(r, H, 0, mine * half_rows, half_rows)
+        return remote(view, view, dd_ss.at[r, H - 1, 0], dd_rs.at[r, H - 1, 0], partner)
+
+    def hand_own(r):
+        return (
+            remote(own_tokens, block(r, H, 1), own_ss.at[0], own_rs.at[0], partner),
+            remote(own_meta, note(r, H, 1), own_ss.at[1], own_rs.at[1], partner),
+        )
+
+    def own_arrival(r):
+        return (
+            remote(block(r, H, 1), block(r, H, 1), own_ss.at[0], own_rs.at[0], partner),
+            remote(note(r, H, 1), note(r, H, 1), own_ss.at[1], own_rs.at[1], partner),
+        )
+
+    @pl.when(c == 0)
+    def _():
+        send_first(0)
+
+    for copy in hand_own(c):
+        copy.start()
     for w in weights:
         w.start()
 
@@ -171,33 +212,76 @@
     col_i = lax.broadcasted_iota(jnp.int32, (4 * T, 4 * T), 1)
     upper[...] = ((row_i < col_i) & (row_i // T == col_i // T)).astype(f32).astype(bf16)
 
-    def forward(t, i):
-        for m in (0, 1):
-
-            @pl.when(t < H)
+    def forward(p, sub, i):
+        r = (p - 1) // K
+        kk = (p - 1) % K + 1
+        t = 2 * kk - 1 + sub
+        last = kk == K
+
+        @pl.when(p <= H)
+        def _():
+            if i == NC:
+                arrival(r, t, i).wait_recv()
+                if sub == 0:
+                    ring(r, t + 1, i).start()
+                else:
+
+                    @pl.when(kk < K)
+                    def _():
+                        ring(r, t + 1, i).start()
+
+            elif sub == 0:
+                arrival(r, t, i).wait_recv()
+
+                @pl.when((kk < K) | (c == i // (NC // 2)))
+                def _():
+                    ring(r, t + 1, i).start()
+
+            else:
+
+                @pl.when((kk < K) | (c == i // (NC // 2)))
+                def _():
+                    arrival(r, t, i).wait_recv()
+
+                @pl.when(kk < K)
+                def _():
+                    ring(r, t + 1, i).start()
+
+            if i == NC - 1:
+                if sub == 0:
+                    for copy in hand(r, t):
+                        copy.start()
+                else:
+
+                    @pl.when(kk < K)
+                    def _():
+                        for copy in hand(r, t):
+                            copy.start()
+
+                    @pl.when(last)
+                    def _():
+                        hand_far(r, c).start()
+
+    def stage1a(k):
+        r = (k - 1) // K
+        kk = (k - 1) % K + 1
+        for copy in hand(r, 2 * kk - 1):
+            copy.wait_recv()
+
+        @pl.when(kk < K)
+        def _():
+            for copy in hand(r, 2 * kk):
+                copy.wait_recv()
+
+        @pl.when(kk == K)
+        def _():
+            hand_far(r, 1 - c).wait_recv()
+
+            @pl.when(c != r)
             def _():
-                ring_arrival(m, t, i).wait_recv()
-                if mine(m, i):
-                    ring(m, t + 1, i).start()
-                else:
-
-                    @pl.when(t + 1 < H)
-                    def _():
-                        ring(m, t + 1, i).start()
-
-                hand(m, t, i).start()
-
-            if mine(m, i):
-
-                @pl.when(t == H)
-                def _():
-                    ring_arrival(m, t, i).wait_recv()
-                    hand(0, t, i).start()
-
-    def stage1a(k):
-        for d in (0, 1):
-            for i in range(NC + 1):
-                hand(d, k, i).wait_recv()
+                for copy in own_arrival(r):
+                    copy.wait_recv()
+
         half = lax.broadcasted_iota(jnp.int32, own_meta.shape, 1) < T
         ids, ws = [], []
         for d in (0, 1):
@@ -319,8 +403,17 @@
             for copy in h_far(k, n, cols, rows, dev):
                 copy.start()
 
-    def give(k, d):
-        return remote(ps.at[k - 1, d], pr.at[k - 1, d], pd_ss.at[k - 1, d], pd_rs.at[k - 1, d], partner)
+    def give(r, k):
+        return remote(ps.at[r, k - 1], pr.at[r, k - 1], pd_ss.at[r, k - 1], pd_rs.at[r, k - 1], partner)
+
+    def give_far(r, theirs):
+        rows = pl.ds(pl.multiple_of(theirs * half_rows, CH), half_rows)
+        return remote(
+            ps.at[r, H - 1, rows], pr.at[r, H - 1, rows], pd_ss.at[r, H - 1], pd_rs.at[r, H - 1], partner
+        )
+
+    def give_home(r):
+        return remote(ps_home.at[r], pr_home.at[r], ph_ss.at[r], ph_rs.at[r], partner)
 
     def stage5(k):
         for n, dev in ((0, x_right), (1, x_left)):
@@ -336,122 +429,191 @@
         o = (o * weight).astype(bf16)
         stacked = jnp.concatenate([o, sdown_ref[...]], axis=0)
         part = jnp.dot(both, stacked, preferred_element_type=f32)
-        for d in (0, 1):
-            con[k - 1, d] = part[2 * d * T : (2 * d + 1) * T]
-            ps[k - 1, d] = part[(2 * d + 1) * T : (2 * d + 2) * T].astype(bf16)
-        for d in (0, 1):
-            give(k, d).start()
+        r = (k - 1) // K
+        kk = (k - 1) % K + 1
+        for n in (0, 1):
+            ps[r, 2 * kk - 2 + n] = part[2 * n * T : (2 * n + 1) * T].astype(bf16)
+            con[r, 2 * kk - 2 + n] = part[(2 * n + 1) * T : (2 * n + 2) * T]
+        give(r, 2 * kk - 1).start()
+
+        @pl.when(kk < K)
+        def _():
+            give(r, 2 * kk).start()
+
+        @pl.when(kk == K)
+        def _():
+            con_far[r] = part[2 * T : 3 * T]
+            ps_home[r] = part[3 * T : 4 * T].astype(bf16)
+            give_far(r, 1 - c).start()
+            give_home(r).start()
 
     def during(k, stage):
         @pl.when((k >= 1) & (k <= H))
         def _():
             stage(k)
 
-    def step(t, _):
-        forward(t, 0)
-        forward(t, NC)
-
-        @pl.when(t == 2)
+    def step(p, _):
+        @pl.when((p == K) & (c == 1))
+        def _():
+            send_first(1)
+
+        forward(p, 0, 0)
+        forward(p, 0, NC)
+        forward(p, 0, 1)
+
+        @pl.when(p == 2)
         def _():
             for w in weights:
                 w.wait()
 
-        during(t - 1, stage1a)
-        forward(t, 1)
-        during(t - 1, stage1b)
-        forward(t, 2)
-        during(t - 5, stage5)
-        forward(t, 3)
-        during(t - 4, stage4)
-        during(t - 3, stage3)
-        during(t - 2, stage2)
+        during(p - 1, stage1a)
+        forward(p, 0, 2)
+        forward(p, 0, 3)
+        during(p - 1, stage1b)
+        forward(p, 1, 0)
+        forward(p, 1, NC)
+        forward(p, 1, 1)
+        during(p - 5, stage5)
+        forward(p, 1, 2)
+        forward(p, 1, 3)
+
+        @pl.when(p >= turn)
+        def _():
+            d = H + turn - p
+
+            @pl.when(d >= 1)
+            def _():
+                back(0, d)
+
+        during(p - 4, stage4)
+        during(p - 3, stage3)
+        during(p - 2, stage2)
         return 0
 
+    def rows(i):
+        return pl.ds(pl.multiple_of(i * CH, CH), CH)
+
+    def pass_on(r, d, i):
+        return remote(
+            rs_s.at[r, d - 1, rows(i)],
+            rs_r.at[r, d - 1, rows(i)],
+            r_ss.at[r, d - 1, i],
+            r_rs.at[r, d - 1, i],
+            z_next,
+        )
+
+    def pass_home(r, i):
+        return remote(
+            rs_s.at[r, 0, rows(i)],
+            fin.at[c, rows(i)],
+            r_ss.at[r, 0, i],
+            f_rs.at[c, i],
+            {"ep": ahead * 2 + r},
+        )
+
+    def own_sum(r, d, i):
+        return con[r, d - 1, rows(i), :] + pr[r, d - 1, rows(i), :].astype(f32)
+
+    def emit(r, d, i, total):
+        rs_s[r, d - 1, rows(i), :] = total.astype(bf16)
+
+        @pl.when(d > 1)
+        def _():
+            pass_on(r, d, i).start()
+
+        @pl.when(d == 1)
+        def _():
+            pass_home(r, i).start()
+
+    def back(r, d):
+        @pl.when(d == H)
+        def _():
+            give_far(r, c).wait_recv()
+            for j in range(NC // 2):
+                i = c * (NC // 2) + j
+                total = con_far[r, rows(i), :] + pr[r, H - 1, rows(i), :].astype(f32)
+                emit(r, d, i, total)
+
+        @pl.when(d < H)
+        def _():
+            give(r, d).wait_recv()
+
+        @pl.when(d == H - 1)
+        def _():
+            for j in range(NC // 2):
+                i = (1 - c) * (NC // 2) + j
+                emit(r, d, i, own_sum(r, d, i))
+            for j in range(NC // 2):
+                i = c * (NC // 2) + j
+                pass_on(r, d + 1, i).wait_recv()
+                emit(r, d, i, own_sum(r, d, i) + rs_r[r, d, rows(i), :].astype(f32))
+
+        @pl.when(d < H - 1)
+        def _():
+            for i in range(NC):
+                pass_on(r, d + 1, i).wait_recv()
+                emit(r, d, i, own_sum(r, d, i) + rs_r[r, d, rows(i), :].astype(f32))
+
     lax.fori_loop(1, H + 6, step, 0)
 
-    def rows(i):
-        return pl.ds(i * CH, CH)
-
-    def pass_on(m, d, i):
-        return remote(
-            rs_s.at[m, d - 1, rows(i)],
-            rs_r.at[m, d - 1, rows(i)],
-            r_ss.at[m, d - 1, i],
-            r_rs.at[m, d - 1, i],
-            z_next[m],
-        )
-
-    def own_sum(d, slot, i):
-        return con[d - 1, slot, rows(i), :] + pr[d - 1, slot, rows(i), :].astype(f32)
-
-    give(H, 0).wait_recv()
+    def rest(n, _):
+        left = turn - 6
+        r = jnp.where(n < left, 0, 1)
+        d = jnp.where(n < left, left - n, H + left - n)
+        back(r, d)
+        return 0
+
+    lax.fori_loop(0, turn - 6 + H, rest, 0)
+    for r in (0, 1):
+        give_home(r).wait_recv()
     for i in range(NC):
-        m = 0 if mine(0, i) else 1
-        rs_s[m, H - 1, rows(i), :] = own_sum(H, 0, i).astype(bf16)
-        pass_on(m, H, i).start()
-
-    def back(d, partly):
-        give(d, 0).wait_recv()
-        give(d, 1).wait_recv()
-        for i in range(NC):
-            for m in (0, 1):
-                total = own_sum(d, 1 - m, i)
-                if not partly or mine(m, i):
-                    pass_on(m, d + 1, i).wait_recv()
-                    total = total + rs_r[m, d, rows(i), :].astype(f32)
-                rs_s[m, d - 1, rows(i), :] = total.astype(bf16)
-                pass_on(m, d, i).start()
-
-    if H > 1:
-        back(H - 1, True)
-
-    def back_step(n, _):
-        back(H - 2 - n, False)
-        return 0
-
-    lax.fori_loop(0, H - 2, back_step, 0)
-    give(H, 1).wait_recv()
-    for i in range(NC):
-        total = own_sum(H, 1, i)
+        total = con[c, H - 1, rows(i), :] + pr_home[c, rows(i), :].astype(f32)
         for m in (0, 1):
-            pass_on(m, 1, i).wait_recv()
-            total = total + rs_r[m, 0, rows(i), :].astype(f32)
+            remote(fin.at[m, rows(i)], fin.at[m, rows(i)], r_ss.at[0, 0, i], f_rs.at[m, i], z_next).wait_recv()
+            total = total + fin[m, rows(i), :].astype(f32)
         out_ref[rows(i), :] = total.astype(bf16)
 
+    for i in range(NC + 1):
+        for m in (0, 1):
+            first_sent(m, i).wait_send()
+    for copy in hand_own(c):
+        copy.wait_send()
+
     def drain(k, _):
-        for i in range(NC + 1):
-            for m in (0, 1):
-                hand(m, k, i).wait_send()
-
-                @pl.when(k < H)
-                def _():
-                    ring_arrival(m, k, i).wait_send()
-
-                if mine(m, i):
-
-                    @pl.when(k == H)
-                    def _():
-                        ring_arrival(m, k, i).wait_send()
+        for r in (0, 1):
+
+            @pl.when(k < H)
+            def _():
+                for copy in hand(r, k):
+                    copy.wait_send()
+                give(r, k).wait_send()
+                for i in range(NC):
+                    pass_on(r, k, i).wait_send()
+
+            @pl.when((k > 1) & (k < H))
+            def _():
+                for i in range(NC):
+                    arrival(r, k, i).wait_send()
+
+            @pl.when(k > 1)
+            def _():
+                arrival(r, k, NC).wait_send()
+
+            @pl.when(k == H)
+            def _():
+                hand_far(r, c).wait_send()
+                give_far(r, 1 - c).wait_send()
+                give_home(r).wait_send()
+                for j in range(NC // 2):
+                    i = c * (NC // 2) + j
+                    arrival(r, k, i).wait_send()
+                    pass_on(r, k, i).wait_send()
 
         for copy in x_first(k) + x_second(k):
             copy.wait_send()
         for n, dev in ((0, x_right), (1, x_left)):
             for copy in h_copy(k, n, own_cols, own_rows, dev) + h_far(k, n, own_cols, own_rows, dev):
                 copy.wait_send()
-            give(k, n).wait_send()
-        for i in range(NC):
-            for m in (0, 1):
-
-                @pl.when(k < H)
-                def _():
-                    pass_on(m, k, i).wait_send()
-
-                if mine(m, i):
-
-                    @pl.when(k == H)
-                    def _():
-                        pass_on(m, k, i).wait_send()
-
         return 0
 
     lax.fori_loop(1, H + 1, drain, 0)
@@ -503,15 +665,21 @@
         vmem((H, 2, UQ, 4 * T), f32),
         vmem((H, R, hidden), bf16),
         vmem((H, units, 4 * T), f32),
-        vmem((H, 2, T, Q), f32),
-        vmem((H, 2, T, Q), bf16),
-        vmem((H, 2, T, Q), bf16),
+        vmem((2, H, T, Q), f32),
         vmem((2, H, T, Q), bf16),
         vmem((2, H, T, Q), bf16),
+        vmem((2, T, Q), f32),
+        vmem((2, T, Q), bf16),
+        vmem((2, T, Q), bf16),
+        vmem((2, H, T, Q), bf16),
+        vmem((2, H, T, Q), bf16),
+        vmem((2, T, Q), bf16),
         dma((7,)),
     ]
-    for shape in ((2, H, NC + 1), (2, H, NC + 1), (H, 8), (H, 4), (H, 4), (H, 4), (H, 2), (2, H, NC)):
+    scratch += [dma((2, H, NC + 1)), dma((2, H, NC + 1)), dma((2, NC + 1))]
+    for shape in ((2,), (2, H, 2), (H, 8), (H, 4), (H, 4), (H, 4), (2, H), (2,), (2, H, NC)):
         scratch += [dma(shape), dma(shape)]
+    scratch.append(dma((2, NC)))
     return pl.pallas_call(
         functools.partial(layer_kernel, (nz, nsub, cap, units)),
         out_shape=jax.ShapeDtypeStruct((T, Q), bf16),

time: 147 us -> 159 us (1.082)
  Pallas kernels: 145 us -> 157 us
    pallas_call x1, Pallas kernels: 145 us -> 157 us  [per_device(): pl.pallas_call(functools.partial(layer_kernel, (nz, nsub, cap, units)), o...]
where the time goes in v3:
time: 159 us
  Pallas kernels  157 us (99%)
  local copies, waits for them, and re-layouts  1.64 us (1%)
    pallas_call x1, Pallas kernels, per_device(): pl.pallas_call(functools.partial(layer_kernel, (nz, nsub, cap, units)), o...  157 us

profile of v3, /device:TPU:33, one launch (start us, length us, event | category | flops | bytes accessed | tf_op | source)
XLA Modules:
  0.0 159.1 jit_solution(10629433911336043038)
XLA Ops:
  0.0 157.4 %shard_map.91 = bf16[64,1792]{1,0:T(8,128)(2,1)} custom-call(s32[8,64]{1,0:T(8,128)} %bitcast.8, f32[8,64]{1,0:T(8,128)} %bitcast.9, bf16[64,1792]{1,0:T(8,128)(2,1)} %tokens_hbm.1, bf16[32,1792]{1,0:T(8,128)(2,1)} %sgate_hbm.1, bf16[32,1792]{1,0:T(8,128)(2,1)} %sup_hbm.1, bf16[32,1792]{1,0:T(8,128)(2,1)} %sdown_hbm.1, bf16[1792,1024]{1,0:T(8,128)(2,1)} %bitcast.5, ...), custom_call_target="tpu_custom_call" | custom-call | tf_op jit(solution)/shard_map/pallas_call | solution.py:683
  157.4 1.6 %copy.11 = bf16[64,1792]{1,0:T(8,128)(2,1)} copy(bf16[64,1792]{1,0:T(8,128)(2,1)} %shard_map.91) | data formatting | bytes 458752

commit v4 on v2

--- a/solution.py
+++ b/solution.py
@@ -237,18 +237,22 @@
     def stage1b(k):
         rows = comp[...]
 
+        first = x_first(k)
         ga = jnp.dot(rows, gate_v[...], preferred_element_type=f32).astype(bf16)
+        for j in range(nsub):
+            xs[k - 1, j, 0] = ga[:, j * HQ : (j + 1) * HQ]
+        first[0].start()
         ua = jnp.dot(rows, up_v[...], preferred_element_type=f32).astype(bf16)
         for j in range(nsub):
-            xs[k - 1, j, 0] = ga[:, j * HQ : (j + 1) * HQ]
             xs[k - 1, j, 1] = ua[:, j * HQ : (j + 1) * HQ]
+        first[1].start()
         contract = (((1,), (1,)), ((), ()))
         pre = lax.dot_general(sgate_ref[...], tok[k - 1], contract, preferred_element_type=f32)
         lin = lax.dot_general(sup_ref[...], tok[k - 1], contract, preferred_element_type=f32)
         for j in range(nsub):
             ss[k - 1, j, 0] = pre[j * UQ : (j + 1) * UQ]
             ss[k - 1, j, 1] = lin[j * UQ : (j + 1) * UQ]
-        for copy in x_first(k):
+        for copy in first[2:]:
             copy.start()
 
     def x_second(k):
@@ -384,11 +388,48 @@
     def own_sum(d, slot, i):
         return con[d - 1, slot, rows(i), :] + pr[d - 1, slot, rows(i), :].astype(f32)
 
+    def drain(k):
+        for i in range(NC + 1):
+            for m in (0, 1):
+                hand(m, k, i).wait_send()
+
+                @pl.when(k < H)
+                def _():
+                    ring_arrival(m, k, i).wait_send()
+
+                if mine(m, i):
+
+                    @pl.when(k == H)
+                    def _():
+                        ring_arrival(m, k, i).wait_send()
+
+        for copy in x_first(k) + x_second(k):
+            copy.wait_send()
+        for n, dev in ((0, x_right), (1, x_left)):
+            for copy in h_copy(k, n, own_cols, own_rows, dev) + h_far(k, n, own_cols, own_rows, dev):
+                copy.wait_send()
+            give(k, n).wait_send()
+
+    def drain_back(d):
+        for i in range(NC):
+            for m in (0, 1):
+
+                @pl.when(d < H)
+                def _():
+                    pass_on(m, d, i).wait_send()
+
+                if mine(m, i):
+
+                    @pl.when(d == H)
+                    def _():
+                        pass_on(m, d, i).wait_send()
+
     give(H, 0).wait_recv()
     for i in range(NC):
         m = 0 if mine(0, i) else 1
         rs_s[m, H - 1, rows(i), :] = own_sum(H, 0, i).astype(bf16)
         pass_on(m, H, i).start()
+    drain(H)
 
     def back(d, partly):
         give(d, 0).wait_recv()
@@ -401,12 +442,14 @@
                     total = total + rs_r[m, d, rows(i), :].astype(f32)
                 rs_s[m, d - 1, rows(i), :] = total.astype(bf16)
                 pass_on(m, d, i).start()
+        drain(d)
 
     if H > 1:
         back(H - 1, True)
 
     def back_step(n, _):
         back(H - 2 - n, False)
+        drain_back(H - n)
         return 0
 
     lax.fori_loop(0, H - 2, back_step, 0)
@@ -418,43 +461,8 @@
             total = total + rs_r[m, 0, rows(i), :].astype(f32)
         out_ref[rows(i), :] = total.astype(bf16)
 
-    def drain(k, _):
-        for i in range(NC + 1):
-            for m in (0, 1):
-                hand(m, k, i).wait_send()
-
-                @pl.when(k < H)
-                def _():
-                    ring_arrival(m, k, i).wait_send()
-
-                if mine(m, i):
-
-                    @pl.when(k == H)
-                    def _():
-                        ring_arrival(m, k, i).wait_send()
-
-        for copy in x_first(k) + x_second(k):
-            copy.wait_send()
-        for n, dev in ((0, x_right), (1, x_left)):
-            for copy in h_copy(k, n, own_cols, own_rows, dev) + h_far(k, n, own_cols, own_rows, dev):
-                copy.wait_send()
-            give(k, n).wait_send()
-        for i in range(NC):
-            for m in (0, 1):
-
-                @pl.when(k < H)
-                def _():
-                    pass_on(m, k, i).wait_send()
-
-                if mine(m, i):
-
-                    @pl.when(k == H)
-                    def _():
-                        pass_on(m, k, i).wait_send()
-
-        return 0
-
-    lax.fori_loop(1, H + 1, drain, 0)
+    for d in range(1, min(3, H + 1)):
+        drain_back(d)
 
 
 def per_device(

time: 147 us -> 146 us (level)
    pallas_call x1, Pallas kernels: 145 us -> 144 us  [per_device(): pl.pallas_call(functools.partial(layer_kernel, (nz, nsub, cap, units)), o...]
where the time goes in v4:
time: 146 us; the launch traced here: 145 us
  Pallas kernels  144 us (99%)
  local copies, waits for them, and re-layouts  1.64 us (1%)
    pallas_call x1, Pallas kernels, per_device(): pl.pallas_call(functools.partial(layer_kernel, (nz, nsub, cap, units)), o...  144 us

profile of v4, /device:TPU:33, one launch (start us, length us, event | category | flops | bytes accessed | tf_op | source)
XLA Modules:
  0.0 145.4 jit_solution(14976038925862866321)
XLA Ops:
  0.0 143.8 %shard_map.91 = bf16[64,1792]{1,0:T(8,128)(2,1)} custom-call(s32[8,64]{1,0:T(8,128)} %bitcast.8, f32[8,64]{1,0:T(8,128)} %bitcast.9, bf16[64,1792]{1,0:T(8,128)(2,1)} %tokens_hbm.1, bf16[32,1792]{1,0:T(8,128)(2,1)} %sgate_hbm.1, bf16[32,1792]{1,0:T(8,128)(2,1)} %sup_hbm.1, bf16[32,1792]{1,0:T(8,128)(2,1)} %sdown_hbm.1, bf16[1792,1024]{1,0:T(8,128)(2,1)} %bitcast.5, ...), custom_call_target="tpu_custom_call" | custom-call | tf_op jit(solution)/shard_map/pallas_call | solution.py:523
  143.8 1.6 %copy.11 = bf16[64,1792]{1,0:T(8,128)(2,1)} copy(bf16[64,1792]{1,0:T(8,128)(2,1)} %shard_map.91) | data formatting | bytes 458752

commit v5 on v4

--- a/solution.py
+++ b/solution.py
@@ -364,11 +364,11 @@
         forward(t, 1)
         during(t - 1, stage1b)
         forward(t, 2)
-        during(t - 5, stage5)
         forward(t, 3)
         during(t - 4, stage4)
         during(t - 3, stage3)
         during(t - 2, stage2)
+        during(t - 5, stage5)
         return 0
 
     lax.fori_loop(1, H + 6, step, 0)

time: 146 us -> 144 us (0.986)
  Pallas kernels: 144 us -> 142 us
where the time goes in v5:
time: 144 us
  Pallas kernels  142 us (99%)
  local copies, waits for them, and re-layouts  1.64 us (1%)
    pallas_call x1, Pallas kernels, per_device(): pl.pallas_call(functools.partial(layer_kernel, (nz, nsub, cap, units)), o...  142 us

profile of v5, /device:TPU:33, one launch (start us, length us, event | category | flops | bytes accessed | tf_op | source)
XLA Modules:
  0.0 144.1 jit_solution(9774911982937122249)
XLA Ops:
  0.0 142.5 %shard_map.91 = bf16[64,1792]{1,0:T(8,128)(2,1)} custom-call(s32[8,64]{1,0:T(8,128)} %bitcast.8, f32[8,64]{1,0:T(8,128)} %bitcast.9, bf16[64,1792]{1,0:T(8,128)(2,1)} %tokens_hbm.1, bf16[32,1792]{1,0:T(8,128)(2,1)} %sgate_hbm.1, bf16[32,1792]{1,0:T(8,128)(2,1)} %sup_hbm.1, bf16[32,1792]{1,0:T(8,128)(2,1)} %sdown_hbm.1, bf16[1792,1024]{1,0:T(8,128)(2,1)} %bitcast.5, ...), custom_call_target="tpu_custom_call" | custom-call | tf_op jit(solution)/shard_map/pallas_call | solution.py:523
  142.5 1.6 %copy.11 = bf16[64,1792]{1,0:T(8,128)(2,1)} copy(bf16[64,1792]{1,0:T(8,128)(2,1)} %shard_map.91) | data formatting | bytes 458752
